TPU v7x, 128 devices: a whole 4x4x4 slice. The times are simulated.
128 devices in a mesh: dp: 64 (over z, y, x), mp: 2 (over core).
Axes of the slice: x: 4, y: 4, z: 4, core: 2. Of those that a mesh axis runs over, the one named last changes fastest.
Arguments:
- pixels: bfloat16 [128, 512, 768], P(('dp', 'mp')), may hold values from -6 to 6
- counts: int32 [64, 2], P('dp'), may hold values from 128 to 512
- owner: int32 [64, 2], P('dp'), may hold values from 0 to 1, each once within a row
- embed_weight: bfloat16 [768, 1024], P('dp', 'mp'), may hold values from -0.21875 to 0.21875
- w_qkv: bfloat16 [3, 1024, 1024], P(None, 'dp', 'mp'), may hold values from -0.8 to 0.8
- w_out: bfloat16 [1024, 1024], P('mp', 'dp'), may hold values from -0.1875 to 0.1875
- w_up: bfloat16 [1024, 4096], P('dp', 'mp'), may hold values from -0.1875 to 0.1875
- w_down: bfloat16 [4096, 1024], P('mp', 'dp'), may hold values from -0.09375 to 0.09375
- ln1_gain: float32 [1024], replicated, may hold values from 0.25 to 1.75
- ln2_gain: float32 [1024], replicated, may hold values from 0.25 to 1.75
- targets: bfloat16 [64, 2, 512, 1024], P('dp', None, 'mp'), may hold values from -20 to 20
Outputs:
- encoded: bfloat16 [64, 2, 512, 1024], P('dp', None, 'mp')
- mean_loss: float32 [], replicated
Inputs may be any that keep to these rules, and one draw needn't show every extreme that they name: counts[g, r] is the number of valid patches at the start of image g * 2 + r; the remaining patch slots are padding. Each row owner[g, :] is a permutation of 0 to 2 - 1, so every held image is encoded once.
All inputs are finite; a program needn't handle non-finite values.
Results may differ from a plain program's by a relative error of at most 0.014.
Values may be sent and summed in bfloat16 or wider, within the bound.
A program may use at most 128 MiB of HBM per device.

v0:
```python
import jax
import jax.numpy as jnp
from jax import lax
from jax.sharding import Mesh
from jax.sharding import PartitionSpec as P

D = 1024
HEAD = 64
DP = ("dp_0", "dp_1", "dp_2")
DP_MP = ("dp_0", "dp_1", "dp_2", "mp")


def joined_along(tiles, dim):
    dims = list(tiles.shape[1:])
    dims[dim] *= tiles.shape[0]
    return jnp.moveaxis(tiles, 0, dim).reshape(dims)


def one_gather(arrays, axis, dims):
    line = jnp.concatenate([a.reshape(-1) for a in arrays])
    lines, at, finished = (lax.all_gather(line, axis), 0, [])
    for a, dim in zip(arrays, dims):
        tiles = lines[:, at : at + a.size].reshape(-1, *a.shape)
        finished.append(joined_along(tiles, dim))
        at += a.size
    return tuple(finished)


def rows_first(arrays, axis, dims):
    turned = [jnp.moveaxis(a, dim, 0) for a, dim in zip(arrays, dims)]
    both = jnp.concatenate([t.reshape(len(t), -1) for t in turned], axis=1)
    whole, at, finished = (lax.all_gather(both, axis, axis=0, tiled=True), 0, [])
    for t, dim in zip(turned, dims):
        section = whole[:, at : at + t[0].size].reshape(-1, *t.shape[1:])
        finished.append(jnp.moveaxis(section, 0, dim))
        at += t[0].size
    return tuple(finished)


def broadcast(shard, axis, root):
    return lax.dynamic_index_in_dim(lax.all_gather(shard, axis), root, 0, keepdims=False)


def copy_for_each(shard, axis):
    length = lax.axis_size(axis)
    return lax.all_to_all(
        jnp.broadcast_to(shard[None], (length, *shard.shape)), axis, 0, 0, tiled=True
    )


def gathered_copies(shard, axis, dim):
    return joined_along(copy_for_each(shard, axis), dim)


def cut_along(shard, dim, length):
    before, after = (shard.shape[:dim], shard.shape[dim + 1 :])
    return jnp.moveaxis(shard.reshape(*before, length, -1, *after), dim, 0)


def sent_and_summed(shard, axis, dim):
    length = lax.axis_size(axis)
    tiles = lax.all_to_all(cut_along(shard, dim, length), axis, 0, 0, tiled=True)
    return jnp.sum(tiles.astype(jnp.float32), axis=0)


def by_axis(shard, axes):
    for axis in axes:
        shard = lax.psum(shard, axis)
    return shard


def layer_norm(inputs, gains):
    average = jnp.mean(inputs, axis=-1, keepdims=True)
    centred = inputs - average
    spread = jnp.mean(centred * centred, axis=-1, keepdims=True)
    return centred * lax.rsqrt(spread + 1e-06) * gains


def attend(queries, key_rows, value_rows, usable):

    def one_head(operands):
        query_part, key_part, value_part = operands
        scores = jnp.einsum("qd,kd->qk", query_part, key_part, preferred_element_type=jnp.float32)
        scores = jnp.where(usable[None, :], scores, -1e30)
        row_max = jnp.max(scores, axis=-1, keepdims=True)
        expo = jnp.exp(scores - row_max)
        row_sum = jnp.sum(expo, axis=-1)
        mixed = jnp.dot(expo.astype(jnp.bfloat16), value_part, preferred_element_type=jnp.float32)
        return mixed / row_sum[:, None]

    return lax.map(one_head, (queries, key_rows, value_rows))


def attention_heads(queries, key_rows, value_rows, length, patches):
    usable = jnp.arange(patches, dtype=jnp.int32) < length
    quarter = patches // 4

    def limited(extent):

        def branch_fn():
            return attend(queries, key_rows[:, :extent], value_rows[:, :extent], usable[:extent])

        return branch_fn

    return lax.switch(
        (length - 1) // quarter, [limited(quarter * (blocks_used + 1)) for blocks_used in range(4)]
    )


def split_heads(projected, patches, factor):
    width = projected.shape[2]
    heads_here = width // HEAD
    queries = (
        (projected[0] * factor)
        .astype(jnp.bfloat16)
        .reshape(patches, heads_here, HEAD)
        .transpose(1, 0, 2)
    )
    key_rows = (
        projected[1].astype(jnp.bfloat16).reshape(patches, heads_here, HEAD).transpose(1, 0, 2)
    )
    value_rows = (
        projected[2].astype(jnp.bfloat16).reshape(patches, heads_here, HEAD).transpose(1, 0, 2)
    )
    return (queries, key_rows, value_rows)


def on_device(
    pixels, counts, owner, embed_weight, w_qkv, w_out, w_up, w_down, ln1_gain, ln2_gain, targets
):
    picture = pixels[0]
    patches = picture.shape[0]
    group_size = lax.axis_size("mp")
    position = lax.axis_index("mp")
    rows_own = patches // group_size
    order = owner[0]
    lengths_all = counts[0]
    slot_ids = jnp.arange(group_size, dtype=jnp.int32)
    factor = HEAD ** (-0.5)
    embed_cols, up_cols = one_gather((embed_weight, w_up), DP, (0, 0))
    qkv_cols, out_rows, down_rows = rows_first((w_qkv, w_out, w_down), DP, (1, 1, 1))

    def step(slot, carry):
        stored, squares_run, number_run = carry
        root = order[slot]
        length = jnp.sum(jnp.where(slot_ids == root, lengths_all, 0))
        shared = broadcast(picture, "mp", root)
        slab = jnp.dot(shared, embed_cols, preferred_element_type=jnp.float32).astype(jnp.bfloat16)
        tokens = gathered_copies(slab, "mp", 1)
        normed = layer_norm(tokens.astype(jnp.float32), ln1_gain).astype(jnp.bfloat16)
        projected = jnp.einsum("pd,cdh->cph", normed, qkv_cols, preferred_element_type=jnp.float32)
        queries, key_rows, value_rows = split_heads(projected, patches, factor)
        mixture = attention_heads(queries, key_rows, value_rows, length, patches)
        attended = (
            mixture.transpose(1, 0, 2).astype(jnp.bfloat16).reshape(patches, qkv_cols.shape[2])
        )
        attention_rows = sent_and_summed(
            jnp.dot(
                lax.slice_in_dim(attended, 0, rows_own * lax.axis_size("mp"), axis=0),
                out_rows,
                preferred_element_type=jnp.float32,
            ).astype(jnp.bfloat16),
            "mp",
            0,
        )
        own_tokens = lax.dynamic_slice_in_dim(tokens, position * rows_own, rows_own, 0)
        residual = own_tokens.astype(jnp.float32) + attention_rows
        normed_own = layer_norm(residual, ln2_gain).astype(jnp.bfloat16)
        hidden = jax.nn.gelu(
            jnp.dot(
                gathered_copies(normed_own, "mp", 0), up_cols, preferred_element_type=jnp.float32
            ),
            approximate=False,
        ).astype(jnp.bfloat16)
        output = residual + lax.psum_scatter(
            jnp.dot(
                lax.slice_in_dim(hidden, 0, lax.axis_size("mp") * rows_own, axis=0),
                down_rows,
                preferred_element_type=jnp.float32,
            ).astype(jnp.bfloat16),
            "mp",
            scatter_dimension=0,
            tiled=True,
        ).astype(jnp.float32)
        wanted = lax.dynamic_index_in_dim(targets[0], slot, 0, keepdims=False).astype(jnp.float32)
        row_ids = position * rows_own + jnp.arange(rows_own, dtype=jnp.int32)
        kept_rows = row_ids < length
        misfit = output - wanted
        squares_run = squares_run + jnp.sum(jnp.where(kept_rows[:, None], misfit * misfit, 0.0))
        number_run = number_run + jnp.sum(kept_rows.astype(jnp.float32))
        stored = lax.dynamic_update_index_in_dim(stored, output.astype(jnp.bfloat16), slot, 0)
        return (stored, squares_run, number_run)

    start_state = (
        jnp.zeros((group_size, rows_own, D), jnp.bfloat16),
        jnp.zeros((), jnp.float32),
        jnp.zeros((), jnp.float32),
    )
    encoded, squares, number = lax.fori_loop(0, group_size, step, start_state)
    total_squares, total_number = (by_axis(squares, DP_MP), by_axis(number, DP_MP))
    return (encoded[None], total_squares / (D * total_number))


def solution(mesh):
    split = Mesh(mesh.devices.reshape(4, 4, 4, mesh.shape["mp"]), ("dp_0", "dp_1", "dp_2", "mp"))
    return jax.shard_map(
        on_device,
        mesh=split,
        in_specs=(
            P(DP_MP, None, None),
            P(DP, None),
            P(DP, None),
            P(DP, "mp"),
            P(None, DP, "mp"),
            P("mp", DP),
            P(DP, "mp"),
            P("mp", DP),
            P(),
            P(),
            P(DP, None, "mp", None),
        ),
        out_specs=(P(DP, None, "mp", None), P()),
        check_vma=False,
    )
```

profile of v0, /device:TPU:1, one launch (start us, length us, event | category | flops | bytes accessed | tf_op | source)
XLA Modules:
  0.0 418.0 jit_solution(11098841160835899786)
XLA Ops:
  11.9 70.7 %all-gather.7.cloned.1.call-done = bf16[2490368]{0:T(1024)(128)(2,1)} async-done(((bf16[38912]{0:T(1024)(128)(2,1)}), bf16[2490368]{0:T(1024)(128)(2,1)}) %all-gather.7.cloned.1.call-update) | async-done | bytes 4980752 | tf_op jit(solution)/shard_map/all_gather | solution.py:21
  82.6 7.8 %reshape.169 = bf16[64,38912]{1,0:T(8,128)(2,1)} reshape(bf16[2490368]{0:T(1024)(128)(2,1)} %all-gather.7.cloned.1.call-done) | data formatting | bytes 9961472 | tf_op jit(solution)/shard_map/all_gather | solution.py:21
  90.4 4.5 %slice.91 = bf16[64,32768]{1,0:T(8,128)(2,1)} slice(bf16[64,38912]{1,0:T(8,128)(2,1)} %reshape.169), slice={[0:64], [6144:38912]} | slice | bytes 8388608 | tf_op jit(solution)/shard_map/slice | solution.py:23
  94.9 7.5 %reshape_reshape.7 = bf16[1024,2048]{1,0:T(8,128)(2,1)} reshape(bf16[64,32768]{1,0:T(8,128)(2,1)} %slice.91) | data formatting | bytes 8388608 | tf_op jit(solution)/shard_map/reshape;reshape | solution.py:16
  104.3 58.3 %all-gather.5.cloned.1.call-done = bf16[1024,4096]{1,0:T(8,128)(2,1)} async-done(((bf16[16,4096]{1,0:T(8,128)(2,1)}), bf16[1024,4096]{1,0:T(8,128)(2,1)}) %all-gather.5.cloned.1.call-update) | async-done | bytes 8388624 | tf_op jit(solution)/shard_map/all_gather | solution.py:32
  162.6 4.7 %slice_bitcast_fusion = bf16[2048,1024]{0,1:T(8,128)(2,1)} fusion(bf16[1024,4096]{1,0:T(8,128)(2,1)} %all-gather.5.cloned.1.call-done), kind=kLoop, calls=%fused_computation.154 | loop fusion | bytes 8388608 | tf_op jit(solution)/shard_map/transpose | solution.py:35
  167.3 6.4 %copy.34 = bf16[2048,1024]{1,0:T(8,128)(2,1)} copy(bf16[2048,1024]{0,1:T(8,128)(2,1)} %slice_bitcast_fusion) | data formatting | bytes 8388608
  175.6 2.9 copy.35
  181.2 189.8 %while.61 = (s32[]{:T(128)}, bf16[2,256,1024]{2,1,0:T(8,128)(2,1)}, f32[]{:T(128)}, f32[]{:T(128)}, bf16[1,512,768]{2,1,0:T(8,128)(2,1)}, /*index=5*/s32[2]{0:T(...) while((s32[]{:T(128)}, bf16[2,256,1024]{2,1,0:T(8,128)(2,1)}, ...), condition=%wide.region_30.31_spmd.clone, body=%wide.region_0.30_spmd.clone.sunk | while | flops 6996395008 | bytes 102745624 | solution.py:199
  187.4 9.2 %all-gather.9.cloned.1.call-done = bf16[2,512,768]{2,1,0:T(8,128)(2,1)} async-done(((bf16[1,512,768]{2,1,0:T(8,128)(2,1)}), bf16[2,512,768]{2,1,0:T(8,128)(2,1)}) %all-gather.9.cloned.1.call-update) | async-done | bytes 1572880 | tf_op jit(solution)/shard_map/while/body/eval_jaxpr/all_gather | solution.py:41
  198.4 4.7 %all_to_all.45 = bf16[2,512,512]{2,1,0:T(8,128)(2,1)S(1)} all-to-all(bf16[2,512,512]{2,1,0:T(8,128)(2,1)S(1)} %broadcast_in_dim.226), channel_id=1, replica_groups=mesh['dp_0'=4,'dp_1'=4,'dp_2'=4,'mp'=2] {'mp'}, dimensions={0} | all-to-all | bytes 2097152 | tf_op jit(solution)/shard_map/while/body/eval_jaxpr/all_to_all | solution.py:46
  203.9 3.7 fusion.186
  212.3 11.5 %conditional.3 = (bf16[8,512,64]{1,2,0:T(8,128)(2,1)}) conditional(s32[]{:T(128)} %clamp.13, (bf16[8,512,64]{2,1,0:T(8,128)(2,1)S(1)}, bf16[8,512,64]{2,1,0:T(8,128)(2,1)S(1)}, pred[512]{0:T(512)(128)(4,1)S(1)}, bf16[8,512,64]{2,1,0:T(8,128)(2,1)S(1)}) %tuple.173, (bf16[8,512,64]{2,1,0:T(8,128)(2,1)S(1)}, ...), branch_computations={%region_4.8_spmd, %region_9.13_spmd, %region_14.18_spmd, %region_1... | conditional | flops 68713472 | bytes 6501041 | solution.py:105
  212.4 11.5 %while.60 = (s32[]{:T(128)}, bf16[8,512,64]{1,2,0:T(8,128)(2,1)}, pred[512]{0:T(512)(128)(4,1)S(1)}, bf16[8,512,64]{2,1,0:T(8,128)(2,1)S(1)}, bf16[8,512,64]{2,1...) while((s32[]{:T(128)}, bf16[8,512,64]{1,2,0:T(8,128)(2,1)}, ...), condition=%wide.region_23.22_spmd, body=%wide.region_20.21_spmd.sunk | while | flops 68713472 | bytes 3682893 | solution.py:91
  223.8 2.2 convolution_convert_fusion.5
  226.0 4.6 %all_to_all.46 = bf16[2,256,1024]{2,1,0:T(8,128)(2,1)S(1)} all-to-all(bf16[2,256,1024]{2,1,0:T(8,128)(2,1)S(1)} %bitcast.229), channel_id=1, replica_groups=mesh['dp_0'=4,'dp_1'=4,'dp_2'=4,'mp'=2] {'mp'}, dimensions={0} | all-to-all | bytes 2097152 | tf_op jit(solution)/shard_map/while/body/eval_jaxpr/all_to_all | solution.py:62
  231.7 4.6 %all_to_all.47 = bf16[2,256,1024]{2,1,0:T(8,128)(2,1)S(1)} all-to-all(bf16[2,256,1024]{2,1,0:T(8,128)(2,1)S(1)} %broadcast_in_dim.227), channel_id=1, replica_groups=mesh['dp_0'=4,'dp_1'=4,'dp_2'=4,'mp'=2] {'mp'}, dimensions={0} | all-to-all | bytes 2097152 | tf_op jit(solution)/shard_map/while/body/eval_jaxpr/all_to_all | solution.py:46
  236.2 16.4 %fusion.190 = bf16[512,1024]{1,0:T(8,128)(2,1)} fusion(bf16[2048,1024]{1,0:T(8,128)(2,1)} %get-tuple-element.1257, bf16[512,1024]{1,0:T(8,128)(2,1)S(1)} %bitcast.230, bf16[1024,2048]{1,0:T(8,128)(2,1)} %get-tuple-element.1256), kind=kOutput, calls=%fused_computation.92.clone.1 | convolution fusion | flops 4363649024 | bytes 10485760 | tf_op jit(solution)/shard_map/while/body/eval_jaxpr/dot_general | solution.py:176
  254.8 16.1 %reduce-scatter.2.cloned.1.call-done = bf16[256,1024]{1,0:T(8,128)(2,1)} async-done(((bf16[512,1024]{1,0:T(8,128)(2,1)}), bf16[256,1024]{1,0:T(8,128)(2,1)}) %reduce-scatter.2.cloned.1.call-update) | async-done | bytes 524304 | tf_op jit(solution)/shard_map/while/body/eval_jaxpr/reduce_scatter | solution.py:175
  281.5 10.3 %all-gather.9.cloned.1.call-done = bf16[2,512,768]{2,1,0:T(8,128)(2,1)} async-done(((bf16[1,512,768]{2,1,0:T(8,128)(2,1)}), bf16[2,512,768]{2,1,0:T(8,128)(2,1)}) %all-gather.9.cloned.1.call-update) | async-done | bytes 1572880 | tf_op jit(solution)/shard_map/while/body/eval_jaxpr/all_gather | solution.py:41
  293.6 4.7 %all_to_all.45 = bf16[2,512,512]{2,1,0:T(8,128)(2,1)S(1)} all-to-all(bf16[2,512,512]{2,1,0:T(8,128)(2,1)S(1)} %broadcast_in_dim.226), channel_id=1, replica_groups=mesh['dp_0'=4,'dp_1'=4,'dp_2'=4,'mp'=2] {'mp'}, dimensions={0} | all-to-all | bytes 2097152 | tf_op jit(solution)/shard_map/while/body/eval_jaxpr/all_to_all | solution.py:46
  299.1 3.7 fusion.186
  307.6 11.5 %conditional.3 = (bf16[8,512,64]{1,2,0:T(8,128)(2,1)}) conditional(s32[]{:T(128)} %clamp.13, (bf16[8,512,64]{2,1,0:T(8,128)(2,1)S(1)}, bf16[8,512,64]{2,1,0:T(8,128)(2,1)S(1)}, pred[512]{0:T(512)(128)(4,1)S(1)}, bf16[8,512,64]{2,1,0:T(8,128)(2,1)S(1)}) %tuple.173, (bf16[8,512,64]{2,1,0:T(8,128)(2,1)S(1)}, ...), branch_computations={%region_4.8_spmd, %region_9.13_spmd, %region_14.18_spmd, %region_1... | conditional | flops 68713472 | bytes 6501041 | solution.py:105
  307.6 11.5 %while.60 = (s32[]{:T(128)}, bf16[8,512,64]{1,2,0:T(8,128)(2,1)}, pred[512]{0:T(512)(128)(4,1)S(1)}, bf16[8,512,64]{2,1,0:T(8,128)(2,1)S(1)}, bf16[8,512,64]{2,1...) while((s32[]{:T(128)}, bf16[8,512,64]{1,2,0:T(8,128)(2,1)}, ...), condition=%wide.region_23.22_spmd, body=%wide.region_20.21_spmd.sunk | while | flops 68713472 | bytes 3682893 | solution.py:91
  321.3 4.6 %all_to_all.46 = bf16[2,256,1024]{2,1,0:T(8,128)(2,1)S(1)} all-to-all(bf16[2,256,1024]{2,1,0:T(8,128)(2,1)S(1)} %bitcast.229), channel_id=1, replica_groups=mesh['dp_0'=4,'dp_1'=4,'dp_2'=4,'mp'=2] {'mp'}, dimensions={0} | all-to-all | bytes 2097152 | tf_op jit(solution)/shard_map/while/body/eval_jaxpr/all_to_all | solution.py:62
  326.9 4.6 %all_to_all.47 = bf16[2,256,1024]{2,1,0:T(8,128)(2,1)S(1)} all-to-all(bf16[2,256,1024]{2,1,0:T(8,128)(2,1)S(1)} %broadcast_in_dim.227), channel_id=1, replica_groups=mesh['dp_0'=4,'dp_1'=4,'dp_2'=4,'mp'=2] {'mp'}, dimensions={0} | all-to-all | bytes 2097152 | tf_op jit(solution)/shard_map/while/body/eval_jaxpr/all_to_all | solution.py:46
  331.5 16.4 %fusion.190 = bf16[512,1024]{1,0:T(8,128)(2,1)} fusion(bf16[2048,1024]{1,0:T(8,128)(2,1)} %get-tuple-element.1257, bf16[512,1024]{1,0:T(8,128)(2,1)S(1)} %bitcast.230, bf16[1024,2048]{1,0:T(8,128)(2,1)} %get-tuple-element.1256), kind=kOutput, calls=%fused_computation.92.clone.1 | convolution fusion | flops 4363649024 | bytes 10485760 | tf_op jit(solution)/shard_map/while/body/eval_jaxpr/dot_general | solution.py:176
  350.0 16.2 %reduce-scatter.2.cloned.1.call-done = bf16[256,1024]{1,0:T(8,128)(2,1)} async-done(((bf16[512,1024]{1,0:T(8,128)(2,1)}), bf16[256,1024]{1,0:T(8,128)(2,1)}) %reduce-scatter.2.cloned.1.call-update) | async-done | bytes 524304 | tf_op jit(solution)/shard_map/while/body/eval_jaxpr/reduce_scatter | solution.py:175
  371.1 10.5 %all-reduce.2 = (f32[]{:T(128)}, f32[]{:T(128)}) all-reduce(f32[]{:T(128)} %get-tuple-element.1279, f32[]{:T(128)} %get-tuple-element.1280), channel_id=1, replica_groups=mesh['dp_0'=4,'dp_1'=4,'dp_2'=4,'mp'=2] {'dp_0'}, use_global_device_ids=true, to_apply=%region_31.32 | all-reduce | flops 2 | bytes 16 | tf_op jit(solution)/shard_map/psum | solution.py:68
  381.6 9.1 %all-reduce.1 = (f32[]{:T(128)}, f32[]{:T(128)}) all-reduce(f32[]{:T(128)} %get-tuple-element.808, f32[]{:T(128)} %get-tuple-element.809), channel_id=1, replica_groups=mesh['dp_0'=4,'dp_1'=4,'dp_2'=4,'mp'=2] {'dp_1'}, use_global_device_ids=true, to_apply=%region_32.33 | all-reduce | flops 2 | bytes 16 | tf_op jit(solution)/shard_map/psum | solution.py:68
  390.6 9.1 %all-reduce = (f32[]{:T(128)}, f32[]{:T(128)}) all-reduce(f32[]{:T(128)} %get-tuple-element.806, f32[]{:T(128)} %get-tuple-element.807), channel_id=1, replica_groups=mesh['dp_0'=4,'dp_1'=4,'dp_2'=4,'mp'=2] {'dp_2'}, use_global_device_ids=true, to_apply=%region_33.34 | all-reduce | flops 2 | bytes 16 | tf_op jit(solution)/shard_map/psum | solution.py:68
  399.7 9.1 %all-reduce.3 = (f32[]{:T(128)}, f32[]{:T(128)}) all-reduce(f32[]{:T(128)} %get-tuple-element.804, f32[]{:T(128)} %get-tuple-element.805), channel_id=1, replica_groups=mesh['dp_0'=4,'dp_1'=4,'dp_2'=4,'mp'=2] {'mp'}, use_global_device_ids=true, to_apply=%region_34.35 | all-reduce | flops 2 | bytes 16 | tf_op jit(solution)/shard_map/psum | solution.py:68
  (156 shorter events, 70.2 us)
Async XLA Ops:
  7.2 75.4 %all-gather.7.cloned.1.call-start = ((), (), s32[]{:S(2)}) async-start(), calls=%async_computation.5 | async-start | bytes 5058560 | tf_op jit(solution)/shard_map/all_gather | solution.py:21
  9.5 153.1 %all-gather.5.cloned.1.call-start = ((), (), s32[]{:S(2)}) async-start(), calls=%async_computation.4 | async-start | bytes 8519680 | tf_op jit(solution)/shard_map/all_gather | solution.py:32
  94.9 7.5 %slice-start = ((bf16[64,38912]{1,0:T(8,128)(2,1)}), bf16[64,6144]{1,0:T(8,128)(2,1)S(1)}, s32[]{:S(2)}) async-start(bf16[64,38912]{1,0:T(8,128)(2,1)} %reshape.169), calls=%async_computation.8 | async-start | bytes 1572864 | tf_op jit(solution)/shard_map/slice | solution.py:23
  173.7 1.9 slice-start.1
  175.6 5.6 %copy-start.6 = (f32[1024]{0:T(1024)S(1)}, f32[1024]{0:T(1024)}, u32[]{:S(2)}) copy-start(f32[1024]{0:T(1024)} %param.34) | copy-start | bytes 12292
  175.6 5.6 %copy-start.8 = (f32[1024]{0:T(1024)S(1)}, f32[1024]{0:T(1024)}, u32[]{:S(2)}) copy-start(f32[1024]{0:T(1024)} %param.33) | copy-start | bytes 12292
  175.6 5.6 %copy-start.9 = (s32[1,2]{1,0:T(1,128)S(1)}, s32[1,2]{1,0:T(1,128)}, u32[]{:S(2)}) copy-start(s32[1,2]{1,0:T(1,128)} %param.27) | copy-start | bytes 28
  175.6 5.6 %copy-start.10 = (s32[1,2]{1,0:T(1,128)S(1)}, s32[1,2]{1,0:T(1,128)}, u32[]{:S(2)}) copy-start(s32[1,2]{1,0:T(1,128)} %param.26) | copy-start | bytes 28
  178.5 2.7 copy-start.4
  181.4 15.2 %all-gather.9.cloned.1.call-start = ((), (), s32[]{:S(2)}) async-start(), calls=%async_computation.6 | async-start | bytes 2359296 | tf_op jit(solution)/shard_map/while/body/eval_jaxpr/all_gather | solution.py:41
  182.2 88.7 %reduce-scatter.2.cloned.1.call-start = ((), (), s32[]{:S(2)}) async-start(), calls=%async_computation.7 | async-start | bytes 1572864 | tf_op jit(solution)/shard_map/while/body/eval_jaxpr/reduce_scatter | solution.py:175
  198.3 5.6 %copy-start.3 = (bf16[3,1024,512]{1,2,0:T(8,128)(2,1)S(1)}, bf16[3,1024,512]{1,2,0:T(8,128)(2,1)}, u32[]{:S(2)}) copy-start(bf16[3,1024,512]{1,2,0:T(8,128)(2,1)} %get-tuple-element.1253) | copy-start | bytes 9437188 | tf_op jit(solution)/shard_map/while
  203.9 3.7 copy-start
  223.8 7.0 %copy-start.1 = (bf16[2,64,8,512]{3,2,0,1:T(8,128)(2,1)S(1)}, bf16[2,64,8,512]{3,2,0,1:T(8,128)(2,1)}, u32[]{:S(2)}) copy-start(bf16[2,64,8,512]{3,2,0,1:T(8,128)(2,1)} %copy-done) | copy-start | bytes 3145732 | tf_op jit(solution)/shard_map/while
  236.2 34.7 %copy-start.2 = (bf16[1,2,256,1024]{3,2,1,0:T(8,128)(2,1)S(1)}, bf16[1,2,256,1024]{3,2,1,0:T(8,128)(2,1)}, u32[]{:S(2)}) copy-start(bf16[1,2,256,1024]{3,2,1,0:T(8,128)(2,1)} %get-tuple-element.1259) | copy-start | bytes 3145732 | tf_op jit(solution)/shard_map/while
  252.7 23.1 %copy-start.5 = (bf16[768,512]{1,0:T(8,128)(2,1)S(1)}, bf16[768,512]{1,0:T(8,128)(2,1)}, u32[]{:S(2)}) copy-start(bf16[768,512]{1,0:T(8,128)(2,1)} %get-tuple-element.1301) | copy-start | bytes 2359300 | tf_op jit(solution)/shard_map/while
  275.8 16.1 %all-gather.9.cloned.1.call-start = ((), (), s32[]{:S(2)}) async-start(), calls=%async_computation.6 | async-start | bytes 2359296 | tf_op jit(solution)/shard_map/while/body/eval_jaxpr/all_gather | solution.py:41
  276.3 89.9 %reduce-scatter.2.cloned.1.call-start = ((), (), s32[]{:S(2)}) async-start(), calls=%async_computation.7 | async-start | bytes 1572864 | tf_op jit(solution)/shard_map/while/body/eval_jaxpr/reduce_scatter | solution.py:175
  293.6 5.6 %copy-start.3 = (bf16[3,1024,512]{1,2,0:T(8,128)(2,1)S(1)}, bf16[3,1024,512]{1,2,0:T(8,128)(2,1)}, u32[]{:S(2)}) copy-start(bf16[3,1024,512]{1,2,0:T(8,128)(2,1)} %get-tuple-element.1253) | copy-start | bytes 9437188 | tf_op jit(solution)/shard_map/while
  299.1 3.7 copy-start
  319.1 7.0 %copy-start.1 = (bf16[2,64,8,512]{3,2,0,1:T(8,128)(2,1)S(1)}, bf16[2,64,8,512]{3,2,0,1:T(8,128)(2,1)}, u32[]{:S(2)}) copy-start(bf16[2,64,8,512]{3,2,0,1:T(8,128)(2,1)} %copy-done) | copy-start | bytes 3145732 | tf_op jit(solution)/shard_map/while
  331.5 34.8 %copy-start.2 = (bf16[1,2,256,1024]{3,2,1,0:T(8,128)(2,1)S(1)}, bf16[1,2,256,1024]{3,2,1,0:T(8,128)(2,1)}, u32[]{:S(2)}) copy-start(bf16[1,2,256,1024]{3,2,1,0:T(8,128)(2,1)} %get-tuple-element.1259) | copy-start | bytes 3145732 | tf_op jit(solution)/shard_map/while
  347.9 23.2 %copy-start.5 = (bf16[768,512]{1,0:T(8,128)(2,1)S(1)}, bf16[768,512]{1,0:T(8,128)(2,1)}, u32[]{:S(2)}) copy-start(bf16[768,512]{1,0:T(8,128)(2,1)} %get-tuple-element.1301) | copy-start | bytes 2359300 | tf_op jit(solution)/shard_map/while
Sparse Core Ops, SparseCore 0:
  10.7 71.7 all-gather.6
  85.5 77.0 all-gather.4
  183.9 12.6 all-gather.8
  252.8 18.0 reduce-scatter.1
  277.9 13.9 all-gather.8
  348.1 18.1 reduce-scatter.1
where the time goes:
time: 421 us; the launch traced here: 418 us
  waiting for transfers between devices  182 us (43%)
  matrix products  67.8 us (16%)
  blocking collectives  65.4 us (16%)
  local copies, waits for them, and re-layouts  49.7 us (12%)
  other arithmetic  27.5 us (7%)
  between operations  16.4 us (4%)
  loops' own time  8.66 us (2%)
    all_gather x1, waiting for transfers between devices, one_gather(): lines, at, finished = (lax.all_gather(line, axis), 0, [])  70.7 us
    all_gather x1, waiting for transfers between devices, rows_first(): lax.all_gather(both, axis, axis=0, tiled=True)  58.3 us
    psum x4, blocking collectives, by_axis(): shard = lax.psum(shard, axis)  37.7 us
    dot_general x2, matrix products, step(): jnp.dot(lax.slice_in_dim(hidden, 0, lax.axis_size('mp') * rows_own, axis=...  32.9 us
    reduce_scatter x2, waiting for transfers between devices, step(): lax.psum_scatter(jnp.dot(lax.slice_in_dim(hidden, 0, lax.axis_size('mp')...  32.4 us
    all_gather x2, waiting for transfers between devices, broadcast(): lax.all_gather(shard, axis)  19.6 us
    all_to_all x4, blocking collectives, copy_for_each(): lax.all_to_all(jnp.broadcast_to(shard[None], (length, *shard.shape)), axi...  18.5 us
    dot_general x16, matrix products, one_head(): jnp.dot(expo.astype(jnp.bfloat16), value_part, preferred_element_type=jnp...  14.6 us
  transfers between devices with their start and end apart: 6, of which 6 were waited for; matrix products, arithmetic and copies ran while one was open for 8% of the time, Pallas kernels for 0%

commit v1 on v0

--- a/solution.py
+++ b/solution.py
@@ -29,7 +29,13 @@
 def rows_first(arrays, axis, dims):
     turned = [jnp.moveaxis(a, dim, 0) for a, dim in zip(arrays, dims)]
     both = jnp.concatenate([t.reshape(len(t), -1) for t in turned], axis=1)
-    whole, at, finished = (lax.all_gather(both, axis, axis=0, tiled=True), 0, [])
+    whole, at, finished = (
+        jnp.concatenate(
+            lax.all_to_all(jnp.stack([both] * lax.axis_size(axis)), axis, 0, 0), axis=0
+        ),
+        0,
+        [],
+    )
     for t, dim in zip(turned, dims):
         section = whole[:, at : at + t[0].size].reshape(-1, *t.shape[1:])
         finished.append(jnp.moveaxis(section, 0, dim))

time: 421 us -> 437 us (1.038)
  starting transfers between devices: 0.21 us -> 12.4 us
  local copies, waits for them, and re-layouts: 49.7 us -> 54.1 us
    all_to_all x0 -> x1, waiting for transfers between devices: none -> 118 us  [rows_first(): lax.all_to_all(jnp.stack([both] * lax.axis_size(axis)), axis, 0, 0)]
    all_gather x1 -> x0, waiting for transfers between devices: 58.3 us -> none  [rows_first(): lax.all_gather(both, axis, axis=0, tiled=True)]
    all_gather x1, waiting for transfers between devices: 70.7 us -> 12.4 us  [one_gather(): lines, at, finished = (lax.all_gather(line, axis), 0, [])]
    all_to_all x0 -> x1, starting transfers between devices: none -> 12.2 us  [rows_first(): lax.all_to_all(jnp.stack([both] * lax.axis_size(axis)), axis, 0, 0)]
    unnamed x14 -> x11, local copies, waits for them, and re-layouts: 11.5 us -> 8.62 us
  transfers between devices with their start and end apart: 6 -> 6, of which waited for: 6 -> 6; matrix products, arithmetic and copies ran while one was open for 8% -> 7% of each run, Pallas kernels for 0% -> 0%
where the time goes in v1:
time: 437 us; the launch traced here: 435 us
  waiting for transfers between devices  183 us (42%)
  matrix products  68.3 us (16%)
  blocking collectives  65.5 us (15%)
  local copies, waits for them, and re-layouts  54.1 us (12%)
  other arithmetic  26.7 us (6%)
  between operations  16.2 us (4%)
  starting transfers between devices  12.4 us (3%)
  loops' own time  8.57 us (2%)
    all_to_all x1, waiting for transfers between devices, rows_first(): lax.all_to_all(jnp.stack([both] * lax.axis_size(axis)), axis, 0, 0)  118 us
    psum x4, blocking collectives, by_axis(): shard = lax.psum(shard, axis)  37.8 us
    dot_general x2, matrix products, step(): jnp.dot(lax.slice_in_dim(hidden, 0, lax.axis_size('mp') * rows_own, axis=...  32.9 us
    reduce_scatter x2, waiting for transfers between devices, step(): lax.psum_scatter(jnp.dot(lax.slice_in_dim(hidden, 0, lax.axis_size('mp')...  32.5 us
    all_gather x2, waiting for transfers between devices, broadcast(): lax.all_gather(shard, axis)  18.7 us
    all_to_all x4, blocking collectives, copy_for_each(): lax.all_to_all(jnp.broadcast_to(shard[None], (length, *shard.shape)), axi...  18.5 us
    dot_general x16, matrix products, one_head(): jnp.dot(expo.astype(jnp.bfloat16), value_part, preferred_element_type=jnp...  14.7 us
    all_gather x1, waiting for transfers between devices, one_gather(): lines, at, finished = (lax.all_gather(line, axis), 0, [])  12.4 us
  transfers between devices with their start and end apart: 6, of which 6 were waited for; matrix products, arithmetic and copies ran while one was open for 7% of the time, Pallas kernels for 0%

profile of v1, /device:TPU:1, one launch (start us, length us, event | category | flops | bytes accessed | tf_op | source)
XLA Modules:
  0.0 434.8 jit_solution(11004374082741273283)
XLA Ops:
  11.1 4.3 stack.2
  15.4 12.2 %all-to-all-start.3 = ((bf16[64,16,4096]{2,1,0:T(8,128)(2,1)}), bf16[64,16,4096]{2,1,0:T(8,128)(2,1)}, u32[]{:S(2)}, u32[]{:S(2)}) async-start(bf16[64,16,4096]{2,1,0:T(8,128)(2,1)} %stack.2), calls=%async_computation.4 | async-start | bytes 16777216 | tf_op jit(solution)/shard_map/all_to_all | solution.py:34
  27.6 118.1 %all-to-all-done.3 = bf16[64,16,4096]{2,1,0:T(8,128)(2,1)} async-done(((bf16[64,16,4096]{2,1,0:T(8,128)(2,1)}), bf16[64,16,4096]{2,1,0:T(8,128)(2,1)}, u32[]{:S(2)}, u32[]{:S(2)}) %all-to-all-start.3) | async-done | bytes 8388640 | tf_op jit(solution)/shard_map/all_to_all | solution.py:34
  147.8 4.7 %slice_bitcast_fusion = bf16[2048,1024]{0,1:T(8,128)(2,1)} fusion(bf16[1024,4096]{1,0:T(8,128)(2,1)} %bitcast.21), kind=kLoop, calls=%fused_computation.154 | loop fusion | bytes 8388608 | tf_op jit(solution)/shard_map/transpose | solution.py:41
  152.6 6.4 %copy.39 = bf16[2048,1024]{1,0:T(8,128)(2,1)} copy(bf16[2048,1024]{0,1:T(8,128)(2,1)} %slice_bitcast_fusion) | data formatting | bytes 8388608
  164.5 12.4 %all-gather.4.cloned.1.call-done = bf16[2490368]{0:T(1024)(128)(2,1)} async-done(((bf16[38912]{0:T(1024)(128)(2,1)}), bf16[2490368]{0:T(1024)(128)(2,1)}) %all-gather.4.cloned.1.call-update) | async-done | bytes 4980752 | tf_op jit(solution)/shard_map/all_gather | solution.py:21
  176.9 7.8 %reshape.175 = bf16[64,38912]{1,0:T(8,128)(2,1)} reshape(bf16[2490368]{0:T(1024)(128)(2,1)} %all-gather.4.cloned.1.call-done) | data formatting | bytes 9961472 | tf_op jit(solution)/shard_map/all_gather | solution.py:21
  184.8 4.5 %slice.91 = bf16[64,32768]{1,0:T(8,128)(2,1)} slice(bf16[64,38912]{1,0:T(8,128)(2,1)} %reshape.175), slice={[0:64], [6144:38912]} | slice | bytes 8388608 | tf_op jit(solution)/shard_map/slice | solution.py:23
  189.3 7.5 %reshape_reshape.7 = bf16[1024,2048]{1,0:T(8,128)(2,1)} reshape(bf16[64,32768]{1,0:T(8,128)(2,1)} %slice.91) | data formatting | bytes 8388608 | tf_op jit(solution)/shard_map/reshape;reshape | solution.py:16
  198.6 189.3 %while.61 = (s32[]{:T(128)}, bf16[2,256,1024]{2,1,0:T(8,128)(2,1)}, f32[]{:T(128)}, f32[]{:T(128)}, bf16[1,512,768]{2,1,0:T(8,128)(2,1)}, /*index=5*/s32[2]{0:T(...) while((s32[]{:T(128)}, bf16[2,256,1024]{2,1,0:T(8,128)(2,1)}, ...), condition=%wide.region_30.31_spmd.clone, body=%wide.region_0.30_spmd.clone.sunk | while | flops 6996395008 | bytes 99599864 | solution.py:205
  204.8 8.4 %all-gather.6.cloned.1.call-done = bf16[2,512,768]{2,1,0:T(8,128)(2,1)} async-done(((bf16[1,512,768]{2,1,0:T(8,128)(2,1)}), bf16[2,512,768]{2,1,0:T(8,128)(2,1)}) %all-gather.6.cloned.1.call-update) | async-done | bytes 1572880 | tf_op jit(solution)/shard_map/while/body/eval_jaxpr/all_gather | solution.py:47
  215.2 4.7 %all_to_all.50 = bf16[2,512,512]{2,1,0:T(8,128)(2,1)S(1)} all-to-all(bf16[2,512,512]{2,1,0:T(8,128)(2,1)S(1)} %broadcast_in_dim.226), channel_id=1, replica_groups=mesh['dp_0'=4,'dp_1'=4,'dp_2'=4,'mp'=2] {'mp'}, dimensions={0} | all-to-all | bytes 2097152 | tf_op jit(solution)/shard_map/while/body/eval_jaxpr/all_to_all | solution.py:52
  220.7 3.7 fusion.186
  229.1 11.6 %conditional.3 = (bf16[8,512,64]{1,2,0:T(8,128)(2,1)}) conditional(s32[]{:T(128)} %clamp.13, (bf16[8,512,64]{2,1,0:T(8,128)(2,1)S(1)}, bf16[8,512,64]{2,1,0:T(8,128)(2,1)S(1)}, pred[512]{0:T(512)(128)(4,1)S(1)}, bf16[8,512,64]{2,1,0:T(8,128)(2,1)S(1)}) %tuple.172, (bf16[8,512,64]{2,1,0:T(8,128)(2,1)S(1)}, ...), branch_computations={%region_4.8_spmd, %region_9.13_spmd, %region_14.18_spmd, %region_1... | conditional | flops 68713472 | bytes 6501041 | solution.py:111
  229.1 11.5 %while.60 = (s32[]{:T(128)}, bf16[8,512,64]{1,2,0:T(8,128)(2,1)}, pred[512]{0:T(512)(128)(4,1)S(1)}, bf16[8,512,64]{2,1,0:T(8,128)(2,1)S(1)}, bf16[8,512,64]{2,1...) while((s32[]{:T(128)}, bf16[8,512,64]{1,2,0:T(8,128)(2,1)}, ...), condition=%wide.region_23.22_spmd, body=%wide.region_20.21_spmd.sunk | while | flops 68713472 | bytes 3682893 | solution.py:97
  242.9 4.6 %all_to_all.51 = bf16[2,256,1024]{2,1,0:T(8,128)(2,1)S(1)} all-to-all(bf16[2,256,1024]{2,1,0:T(8,128)(2,1)S(1)} %bitcast.230), channel_id=1, replica_groups=mesh['dp_0'=4,'dp_1'=4,'dp_2'=4,'mp'=2] {'mp'}, dimensions={0} | all-to-all | bytes 2097152 | tf_op jit(solution)/shard_map/while/body/eval_jaxpr/all_to_all | solution.py:68
  248.5 4.6 %all_to_all.52 = bf16[2,256,1024]{2,1,0:T(8,128)(2,1)S(1)} all-to-all(bf16[2,256,1024]{2,1,0:T(8,128)(2,1)S(1)} %broadcast_in_dim.227), channel_id=1, replica_groups=mesh['dp_0'=4,'dp_1'=4,'dp_2'=4,'mp'=2] {'mp'}, dimensions={0} | all-to-all | bytes 2097152 | tf_op jit(solution)/shard_map/while/body/eval_jaxpr/all_to_all | solution.py:52
  253.1 16.4 %fusion.190 = bf16[512,1024]{1,0:T(8,128)(2,1)} fusion(bf16[2048,1024]{1,0:T(8,128)(2,1)} %get-tuple-element.1274, bf16[512,1024]{1,0:T(8,128)(2,1)S(1)} %bitcast.231, bf16[1024,2048]{1,0:T(8,128)(2,1)} %get-tuple-element.1273), kind=kOutput, calls=%fused_computation.92.clone.1 | convolution fusion | flops 4363649024 | bytes 10485760 | tf_op jit(solution)/shard_map/while/body/eval_jaxpr/dot_general | solution.py:182
  271.5 16.2 %reduce-scatter.2.cloned.1.call-done = bf16[256,1024]{1,0:T(8,128)(2,1)} async-done(((bf16[512,1024]{1,0:T(8,128)(2,1)}), bf16[256,1024]{1,0:T(8,128)(2,1)}) %reduce-scatter.2.cloned.1.call-update) | async-done | bytes 524304 | tf_op jit(solution)/shard_map/while/body/eval_jaxpr/reduce_scatter | solution.py:181
  298.3 10.3 %all-gather.6.cloned.1.call-done = bf16[2,512,768]{2,1,0:T(8,128)(2,1)} async-done(((bf16[1,512,768]{2,1,0:T(8,128)(2,1)}), bf16[2,512,768]{2,1,0:T(8,128)(2,1)}) %all-gather.6.cloned.1.call-update) | async-done | bytes 1572880 | tf_op jit(solution)/shard_map/while/body/eval_jaxpr/all_gather | solution.py:47
  310.6 4.7 %all_to_all.50 = bf16[2,512,512]{2,1,0:T(8,128)(2,1)S(1)} all-to-all(bf16[2,512,512]{2,1,0:T(8,128)(2,1)S(1)} %broadcast_in_dim.226), channel_id=1, replica_groups=mesh['dp_0'=4,'dp_1'=4,'dp_2'=4,'mp'=2] {'mp'}, dimensions={0} | all-to-all | bytes 2097152 | tf_op jit(solution)/shard_map/while/body/eval_jaxpr/all_to_all | solution.py:52
  316.1 3.7 fusion.186
  324.5 11.6 %conditional.3 = (bf16[8,512,64]{1,2,0:T(8,128)(2,1)}) conditional(s32[]{:T(128)} %clamp.13, (bf16[8,512,64]{2,1,0:T(8,128)(2,1)S(1)}, bf16[8,512,64]{2,1,0:T(8,128)(2,1)S(1)}, pred[512]{0:T(512)(128)(4,1)S(1)}, bf16[8,512,64]{2,1,0:T(8,128)(2,1)S(1)}) %tuple.172, (bf16[8,512,64]{2,1,0:T(8,128)(2,1)S(1)}, ...), branch_computations={%region_4.8_spmd, %region_9.13_spmd, %region_14.18_spmd, %region_1... | conditional | flops 68713472 | bytes 6501041 | solution.py:111
  324.5 11.5 %while.60 = (s32[]{:T(128)}, bf16[8,512,64]{1,2,0:T(8,128)(2,1)}, pred[512]{0:T(512)(128)(4,1)S(1)}, bf16[8,512,64]{2,1,0:T(8,128)(2,1)S(1)}, bf16[8,512,64]{2,1...) while((s32[]{:T(128)}, bf16[8,512,64]{1,2,0:T(8,128)(2,1)}, ...), condition=%wide.region_23.22_spmd, body=%wide.region_20.21_spmd.sunk | while | flops 68713472 | bytes 3682893 | solution.py:97
  338.3 4.6 %all_to_all.51 = bf16[2,256,1024]{2,1,0:T(8,128)(2,1)S(1)} all-to-all(bf16[2,256,1024]{2,1,0:T(8,128)(2,1)S(1)} %bitcast.230), channel_id=1, replica_groups=mesh['dp_0'=4,'dp_1'=4,'dp_2'=4,'mp'=2] {'mp'}, dimensions={0} | all-to-all | bytes 2097152 | tf_op jit(solution)/shard_map/while/body/eval_jaxpr/all_to_all | solution.py:68
  343.9 4.6 %all_to_all.52 = bf16[2,256,1024]{2,1,0:T(8,128)(2,1)S(1)} all-to-all(bf16[2,256,1024]{2,1,0:T(8,128)(2,1)S(1)} %broadcast_in_dim.227), channel_id=1, replica_groups=mesh['dp_0'=4,'dp_1'=4,'dp_2'=4,'mp'=2] {'mp'}, dimensions={0} | all-to-all | bytes 2097152 | tf_op jit(solution)/shard_map/while/body/eval_jaxpr/all_to_all | solution.py:52
  348.4 16.4 %fusion.190 = bf16[512,1024]{1,0:T(8,128)(2,1)} fusion(bf16[2048,1024]{1,0:T(8,128)(2,1)} %get-tuple-element.1274, bf16[512,1024]{1,0:T(8,128)(2,1)S(1)} %bitcast.231, bf16[1024,2048]{1,0:T(8,128)(2,1)} %get-tuple-element.1273), kind=kOutput, calls=%fused_computation.92.clone.1 | convolution fusion | flops 4363649024 | bytes 10485760 | tf_op jit(solution)/shard_map/while/body/eval_jaxpr/dot_general | solution.py:182
  366.9 16.3 %reduce-scatter.2.cloned.1.call-done = bf16[256,1024]{1,0:T(8,128)(2,1)} async-done(((bf16[512,1024]{1,0:T(8,128)(2,1)}), bf16[256,1024]{1,0:T(8,128)(2,1)}) %reduce-scatter.2.cloned.1.call-update) | async-done | bytes 524304 | tf_op jit(solution)/shard_map/while/body/eval_jaxpr/reduce_scatter | solution.py:181
  387.9 10.5 %all-reduce.2 = (f32[]{:T(128)}, f32[]{:T(128)}) all-reduce(f32[]{:T(128)} %get-tuple-element.650, f32[]{:T(128)} %get-tuple-element.651), channel_id=1, replica_groups=mesh['dp_0'=4,'dp_1'=4,'dp_2'=4,'mp'=2] {'dp_0'}, use_global_device_ids=true, to_apply=%region_31.32 | all-reduce | flops 2 | bytes 16 | tf_op jit(solution)/shard_map/psum | solution.py:74
  398.5 9.1 %all-reduce.1 = (f32[]{:T(128)}, f32[]{:T(128)}) all-reduce(f32[]{:T(128)} %get-tuple-element.825, f32[]{:T(128)} %get-tuple-element.826), channel_id=1, replica_groups=mesh['dp_0'=4,'dp_1'=4,'dp_2'=4,'mp'=2] {'dp_1'}, use_global_device_ids=true, to_apply=%region_32.33 | all-reduce | flops 2 | bytes 16 | tf_op jit(solution)/shard_map/psum | solution.py:74
  407.6 9.0 %all-reduce = (f32[]{:T(128)}, f32[]{:T(128)}) all-reduce(f32[]{:T(128)} %get-tuple-element.823, f32[]{:T(128)} %get-tuple-element.824), channel_id=1, replica_groups=mesh['dp_0'=4,'dp_1'=4,'dp_2'=4,'mp'=2] {'dp_2'}, use_global_device_ids=true, to_apply=%region_33.34 | all-reduce | flops 2 | bytes 16 | tf_op jit(solution)/shard_map/psum | solution.py:74
  416.6 9.2 %all-reduce.3 = (f32[]{:T(128)}, f32[]{:T(128)}) all-reduce(f32[]{:T(128)} %get-tuple-element.821, f32[]{:T(128)} %get-tuple-element.822), channel_id=1, replica_groups=mesh['dp_0'=4,'dp_1'=4,'dp_2'=4,'mp'=2] {'mp'}, use_global_device_ids=true, to_apply=%region_34.35 | all-reduce | flops 2 | bytes 16 | tf_op jit(solution)/shard_map/psum | solution.py:74
  (149 shorter events, 75.1 us)
Async XLA Ops:
  7.2 169.8 %all-gather.4.cloned.1.call-start = ((), (), s32[]{:S(2)}) async-start(), calls=%async_computation.5 | async-start | bytes 5058560 | tf_op jit(solution)/shard_map/all_gather | solution.py:21
  15.4 130.4 %all-to-all-start.3 = ((bf16[64,16,4096]{2,1,0:T(8,128)(2,1)}), bf16[64,16,4096]{2,1,0:T(8,128)(2,1)}, u32[]{:S(2)}, u32[]{:S(2)}) async-start(bf16[64,16,4096]{2,1,0:T(8,128)(2,1)} %stack.2), calls=%async_computation.4 | async-start | bytes 16777216 | tf_op jit(solution)/shard_map/all_to_all | solution.py:34
  189.2 7.5 %slice-start = ((bf16[64,38912]{1,0:T(8,128)(2,1)}), bf16[64,6144]{1,0:T(8,128)(2,1)S(1)}, s32[]{:S(2)}) async-start(bf16[64,38912]{1,0:T(8,128)(2,1)} %reshape.175), calls=%async_computation.8 | async-start | bytes 1572864 | tf_op jit(solution)/shard_map/slice | solution.py:23
  189.2 9.4 %copy-start.4 = (f32[1024]{0:T(1024)S(1)}, f32[1024]{0:T(1024)}, u32[]{:S(2)}) copy-start(f32[1024]{0:T(1024)} %param.34) | copy-start | bytes 12292
  189.2 9.4 %copy-start.6 = (f32[1024]{0:T(1024)S(1)}, f32[1024]{0:T(1024)}, u32[]{:S(2)}) copy-start(f32[1024]{0:T(1024)} %param.33) | copy-start | bytes 12292
  189.2 9.4 %copy-start.7 = (s32[1,2]{1,0:T(1,128)S(1)}, s32[1,2]{1,0:T(1,128)}, u32[]{:S(2)}) copy-start(s32[1,2]{1,0:T(1,128)} %param.27) | copy-start | bytes 28
  189.3 9.4 %copy-start.8 = (s32[1,2]{1,0:T(1,128)S(1)}, s32[1,2]{1,0:T(1,128)}, u32[]{:S(2)}) copy-start(s32[1,2]{1,0:T(1,128)} %param.26) | copy-start | bytes 28
  198.8 14.3 %all-gather.6.cloned.1.call-start = ((), (), s32[]{:S(2)}) async-start(), calls=%async_computation.6 | async-start | bytes 2359296 | tf_op jit(solution)/shard_map/while/body/eval_jaxpr/all_gather | solution.py:47
  199.6 88.2 %reduce-scatter.2.cloned.1.call-start = ((), (), s32[]{:S(2)}) async-start(), calls=%async_computation.7 | async-start | bytes 1572864 | tf_op jit(solution)/shard_map/while/body/eval_jaxpr/reduce_scatter | solution.py:181
  215.1 5.6 %copy-start.3 = (bf16[3,1024,512]{1,2,0:T(8,128)(2,1)S(1)}, bf16[3,1024,512]{1,2,0:T(8,128)(2,1)}, u32[]{:S(2)}) copy-start(bf16[3,1024,512]{1,2,0:T(8,128)(2,1)} %get-tuple-element.1270) | copy-start | bytes 9437188 | tf_op jit(solution)/shard_map/while
  220.7 3.7 copy-start
  240.7 7.0 %copy-start.1 = (bf16[2,64,8,512]{3,2,0,1:T(8,128)(2,1)S(1)}, bf16[2,64,8,512]{3,2,0,1:T(8,128)(2,1)}, u32[]{:S(2)}) copy-start(bf16[2,64,8,512]{3,2,0,1:T(8,128)(2,1)} %copy-done) | copy-start | bytes 3145732 | tf_op jit(solution)/shard_map/while
  253.1 34.7 %copy-start.2 = (bf16[1,2,256,1024]{3,2,1,0:T(8,128)(2,1)S(1)}, bf16[1,2,256,1024]{3,2,1,0:T(8,128)(2,1)}, u32[]{:S(2)}) copy-start(bf16[1,2,256,1024]{3,2,1,0:T(8,128)(2,1)} %get-tuple-element.1276) | copy-start | bytes 3145732 | tf_op jit(solution)/shard_map/while
  292.5 16.1 %all-gather.6.cloned.1.call-start = ((), (), s32[]{:S(2)}) async-start(), calls=%async_computation.6 | async-start | bytes 2359296 | tf_op jit(solution)/shard_map/while/body/eval_jaxpr/all_gather | solution.py:47
  293.1 90.1 %reduce-scatter.2.cloned.1.call-start = ((), (), s32[]{:S(2)}) async-start(), calls=%async_computation.7 | async-start | bytes 1572864 | tf_op jit(solution)/shard_map/while/body/eval_jaxpr/reduce_scatter | solution.py:181
  310.5 5.6 %copy-start.3 = (bf16[3,1024,512]{1,2,0:T(8,128)(2,1)S(1)}, bf16[3,1024,512]{1,2,0:T(8,128)(2,1)}, u32[]{:S(2)}) copy-start(bf16[3,1024,512]{1,2,0:T(8,128)(2,1)} %get-tuple-element.1270) | copy-start | bytes 9437188 | tf_op jit(solution)/shard_map/while
  316.1 3.7 copy-start
  336.0 7.0 %copy-start.1 = (bf16[2,64,8,512]{3,2,0,1:T(8,128)(2,1)S(1)}, bf16[2,64,8,512]{3,2,0,1:T(8,128)(2,1)}, u32[]{:S(2)}) copy-start(bf16[2,64,8,512]{3,2,0,1:T(8,128)(2,1)} %copy-done) | copy-start | bytes 3145732 | tf_op jit(solution)/shard_map/while
  348.4 34.8 %copy-start.2 = (bf16[1,2,256,1024]{3,2,1,0:T(8,128)(2,1)S(1)}, bf16[1,2,256,1024]{3,2,1,0:T(8,128)(2,1)}, u32[]{:S(2)}) copy-start(bf16[1,2,256,1024]{3,2,1,0:T(8,128)(2,1)} %get-tuple-element.1276) | copy-start | bytes 3145732 | tf_op jit(solution)/shard_map/while
Sparse Core Ops, SparseCore 0:
  10.7 166.1 all-gather.3
  201.3 11.8 all-gather.5
  269.6 18.0 reduce-scatter.1
  294.6 13.8 all-gather.5
  365.0 18.1 reduce-scatter.1
